TPU v7x, 8 devices: a whole 2x2x1 slice. The times are simulated.
8 devices in a mesh: dp: 2 (over z, y), ep: 4 (over x, core).
Axes of the slice: x: 2, y: 2, z: 1, core: 2. Of those that a mesh axis runs over, the one named last changes fastest.
Arguments:
- x_in: bfloat16 [1536, 2560], P(('dp', 'ep')), parts along dimension 0
- norm_gain: bfloat16 [2560], replicated
- w_router: bfloat16 [2560, 64], replicated
- expert_ids: int32 [1536, 6], P(('dp', 'ep')), parts along dimension 0
- w_gate: bfloat16 [64, 2560, 1536], P('ep')
- w_up: bfloat16 [64, 2560, 1536], P('ep')
- w_down: bfloat16 [64, 1536, 2560], P('ep')
Outputs:
- output: bfloat16 [1536, 2560], P(('dp', 'ep')), parts along dimension 0
There are 2 independent parts. A program takes and returns all parts, laid end to end along the dimension named above; an argument that names none is the same for every part.
All inputs are finite; a program needn't handle non-finite values.
Results may differ from a plain program's by a relative error of at most 0.001.
Values are sent between devices in bfloat16 or wider.
A program may use at most 1.5 GiB of HBM per device.

v0:
```python
import jax
import jax.numpy as jnp
from jax import lax
from jax.sharding import PartitionSpec as P

EPS = 1e-6


def norm_and_gates(x_in, norm_gain, w_router, expert_ids):
    resid = x_in.astype(jnp.float32)
    mean_sq = jnp.mean(resid * resid, axis=-1, keepdims=True)
    normed = (resid * lax.rsqrt(mean_sq + EPS) * norm_gain.astype(jnp.float32)).astype(jnp.bfloat16)
    logits = jnp.dot(normed, w_router, preferred_element_type=jnp.float32)
    router_p = jax.nn.softmax(logits, axis=-1)
    picked = jnp.take_along_axis(router_p, expert_ids, axis=1)
    gates = picked / jnp.sum(picked, axis=1, keepdims=True)
    return resid, normed, gates


def route_slots(expert_ids, experts, capacity):
    flat_ids = expert_ids.reshape(-1)
    onehot = (flat_ids[:, None] == jnp.arange(experts, dtype=jnp.int32)[None, :]).astype(jnp.int32)
    before = jnp.cumsum(onehot, axis=0) - onehot
    position = jnp.sum(before * onehot, axis=1)
    return flat_ids * capacity + position


def expert_mlp(rows, w_gate, w_up, w_down):
    gate_val = jnp.einsum("erd,edf->erf", rows, w_gate, preferred_element_type=jnp.float32)
    up_val = jnp.einsum("erd,edf->erf", rows, w_up, preferred_element_type=jnp.float32)
    hidden_act = (jax.nn.silu(gate_val) * up_val).astype(jnp.bfloat16)
    return jnp.einsum("erf,efd->erd", hidden_act, w_down, preferred_element_type=jnp.float32).astype(jnp.bfloat16)


def solution(mesh):
    def local_block(x_in, norm_gain, w_router, expert_ids, w_gate, w_up, w_down):
        tokens, hidden = x_in.shape
        experts = w_router.shape[1]
        top_k = expert_ids.shape[1]
        capacity = 2 * tokens * top_k // experts
        resid, normed, gates = norm_and_gates(x_in, norm_gain, w_router, expert_ids)
        slots = route_slots(expert_ids, experts, capacity)
        choice_tok = jnp.arange(tokens * top_k, dtype=jnp.int32) // top_k
        slot_tok = jnp.full((experts * capacity,), tokens, jnp.int32).at[slots].set(choice_tok)
        outgoing = jnp.take(normed, slot_tok, axis=0, mode="fill", fill_value=0).reshape(experts, capacity, hidden)
        received = lax.all_to_all(outgoing, "ep", 0, 1, tiled=True)
        outputs = expert_mlp(received, w_gate, w_up, w_down)
        returned = lax.all_to_all(outputs, "ep", 1, 0, tiled=True).reshape(experts * capacity, hidden)
        y_sel = jnp.take(returned, slots, axis=0).reshape(tokens, top_k, hidden)
        mixed = jnp.sum(y_sel.astype(jnp.float32) * gates[:, :, None], axis=1)
        return (resid + mixed).astype(jnp.bfloat16)

    tok_spec = P(("dp", "ep"), None)
    expert_spec = P("ep", None, None)
    return jax.shard_map(local_block, mesh=mesh, in_specs=(tok_spec, P(None), P(None, None), tok_spec, expert_spec, expert_spec, expert_spec), out_specs=tok_spec, check_vma=False)
```

profile of v0, /device:TPU:0, one launch (start us, length us, event | category | flops | bytes accessed | tf_op | source)
XLA Modules:
  0.0 612.5 jit_solution(9605597471310149494)
XLA Ops:
  0.0 0.0 copy-start
  0.0 0.7 broadcast_multiply_fusion
  0.7 0.8 copy.42
  1.6 0.1 eq.26
  1.7 0.1 reshape.109
  1.9 0.1 copy.48
  2.0 0.1 mul.59
  2.2 18.1 %reduce-window.6 = s32[64,9,128]{2,1,0:T(8,128)S(1)} reduce-window(s32[64,9,128]{2,1,0:T(8,128)S(1)} %fusion.12, s32[]{:T(128)} %constant.44.clone.1), window={size=1x1x128 pad=0_0x0_0x127_0}, to_apply=%region_0.0 | reduce-window | flops 9363456 | bytes 589828 | tf_op jit(solution)/shard_map/reduce-window
  20.3 0.2 slice.14
  20.5 0.3 copy.44
  20.8 0.1 copy.45
  20.9 0.2 broadcast_add_fusion
  21.1 0.1 fusion.15
  21.3 0.0 copy-start.5
  21.3 0.6 copy-done.5
  21.9 6.5 %scatter_custom_fusion = s32[2304]{0:T(1024)S(1)} fusion(s32[1152]{0:T(1024)S(1)} %fusion.23, s32[1152]{0:T(1024)S(1)} %add_select_fusion, s32[]{:T(128)} %constant.47.clone.1), kind=kCustom, calls=%fused_computation.47 | custom fusion | bytes 9220 | tf_op jit(solution)/shard_map/scatter | solution.py:44
  28.4 0.7 convert_element_type.31
  29.1 1.5 fusion.6
  30.6 1.5 fusion.8
  32.1 0.0 copy-start.1
  32.1 10.5 %gather_fusion = bf16[2304,2560]{1,0:T(8,128)(2,1)} fusion(bf16[192,2560]{1,0:T(8,128)(2,1)S(1)} %fusion.8, s32[3072]{0:T(1024)S(1)} %pad_clamp_fusion), kind=kCustom, calls=%fused_computation | custom fusion | bytes 23602176 | tf_op jit(solution)/shard_map/jit(_take)/gather | solution.py:45
  42.7 15.4 %gather.17 = bf16[64,36,2560]{2,1,0:T(8,128)(2,1)} reshape(bf16[2304,2560]{1,0:T(8,128)(2,1)} %gather_fusion) | data formatting | bytes 23592960 | tf_op jit(solution)/shard_map/jit(_take)/gather | solution.py:45
  58.1 0.1 broadcast_in_dim.41
  58.2 6.5 %broadcast_select_fusion = bf16[64,36,2560]{2,1,0:T(8,128)(2,1)S(1)} fusion(bf16[64,36,2560]{2,1,0:T(8,128)(2,1)} %gather.17, pred[64,36]{1,0:T(8,128)(4,1)S(1)} %broadcast_in_dim.41), kind=kLoop, calls=%fused_computation.6 | loop fusion | flops 5898240 | bytes 23595264 | tf_op jit(solution)/shard_map/jit(_take)/select_n | solution.py:45
  64.7 148.1 %all_to_all.33 = bf16[64,36,2560]{2,1,0:T(8,128)(2,1)S(1)} all-to-all(bf16[64,36,2560]{2,1,0:T(8,128)(2,1)S(1)} %broadcast_select_fusion), channel_id=1, replica_groups=mesh['dp'=2,'ep'=4] {'ep'}, dimensions={0} | all-to-all | bytes 23592960 | tf_op jit(solution)/shard_map/all_to_all | solution.py:46
  212.7 9.2 %copy.50 = bf16[16,4,36,2560]{3,0,2,1:T(8,128)(2,1)} copy(bf16[16,4,36,2560]{3,2,0,1:T(8,128)(2,1)S(1)} %bitcast.42) | data formatting | bytes 23592960 | tf_op jit(solution)/shard_map/all_to_all | solution.py:46
  221.9 61.5 %fusion = f32[16,144,1536]{2,1,0:T(8,128)} fusion(bf16[16,2560,1536]{2,1,0:T(8,128)(2,1)} %param.12, bf16[16,144,2560]{2,0,1:T(8,128)(2,1)} %bitcast.40), kind=kOutput, calls=%fused_computation.7 | convolution fusion | flops 18119393280 | bytes 151781376 | tf_op jit(solution)/shard_map/erd,edf->erf/dot_general | solution.py:30
  283.5 62.8 %multiply_convert_fusion.clone.4 = bf16[16,144,1536]{2,1,0:T(8,128)(2,1)} fusion(f32[16,144,1536]{2,1,0:T(8,128)} %fusion, bf16[16,2560,1536]{2,1,0:T(8,128)(2,1)} %param.11, bf16[16,144,2560]{2,0,1:T(8,128)(2,1)} %bitcast.41), kind=kOutput, calls=%fused_computation.5.clone.clone.clone.1 | convolution fusion | flops 18140626944 | bytes 158859264 | tf_op jit(solution)/shard_map/erd,edf->erf/dot_general | solution.py:29
  346.2 47.1 %convolution_convert_fusion = bf16[16,144,2560]{2,1,0:T(8,128)(2,1)} fusion(bf16[16,1536,2560]{2,1,0:T(8,128)(2,1)} %param.13, bf16[16,144,1536]{2,1,0:T(8,128)(2,1)} %multiply_convert_fusion.clone.4), kind=kOutput, calls=%fused_computation.11 | convolution fusion | flops 18125291520 | bytes 144703488 | tf_op jit(solution)/shard_map/erf,efd->erd/dot_general | solution.py:32
  393.4 18.1 %copy.53 = bf16[16,144,2560]{2,0,1:T(8,128)(2,1)} copy(bf16[16,144,2560]{2,1,0:T(8,128)(2,1)} %convolution_convert_fusion) | data formatting | bytes 23592960 | tf_op jit(solution)/shard_map/convert_element_type | solution.py:32
  411.4 6.6 %all-to-all-start.1 = ((bf16[16,144,2560]{2,0,1:T(8,128)(2,1)}), bf16[16,144,2560]{2,0,1:T(8,128)(2,1)}, u32[]{:S(2)}, u32[]{:S(2)}) async-start(bf16[16,144,2560]{2,0,1:T(8,128)(2,1)} %copy.53), calls=%async_computation.1 | async-start | bytes 23592960 | tf_op jit(solution)/shard_map/all_to_all | solution.py:48
  418.0 0.1 reduce_sum.50
  418.2 0.1 copy.55
  418.3 0.1 reshape.129
  418.5 0.4 fusion.26
  419.0 9.3 %gather_fusion.2 = f32[1152]{0:T(1024)S(1)} fusion(f32[192,64]{0,1:T(8,128)S(1)} %fusion.16, s32[1152]{0:T(1024)S(1)} %reshape.129), kind=kCustom, calls=%fused_computation.2 | custom fusion | bytes 18432 | tf_op jit(solution)/shard_map/jit(take_along_axis)/gather | solution.py:15
  428.3 0.1 reshape.132
  428.4 0.1 copy.56
  428.6 0.1 copy.57
  428.7 0.1 copy.46
  428.8 0.2 copy.47
  429.0 118.4 %all-to-all-done.1 = bf16[16,144,2560]{2,0,1:T(8,128)(2,1)} async-done(((bf16[16,144,2560]{2,0,1:T(8,128)(2,1)}), bf16[16,144,2560]{2,0,1:T(8,128)(2,1)}, u32[]{:S(2)}, u32[]{:S(2)}) %all-to-all-start.1) | async-done | bytes 11796512 | tf_op jit(solution)/shard_map/all_to_all | solution.py:48
  547.3 10.0 %copy.54 = bf16[4,16,36,2560]{3,2,1,0:T(8,128)(2,1)} copy(bf16[4,16,36,2560]{3,1,2,0:T(8,128)(2,1)} %bitcast.7) | data formatting | bytes 23592960 | tf_op jit(solution)/shard_map/all_to_all | solution.py:48
  557.3 14.7 %reshape.111 = bf16[2304,2560]{1,0:T(8,128)(2,1)} reshape(bf16[4,16,36,2560]{3,2,1,0:T(8,128)(2,1)} %copy.54) | data formatting | bytes 23592960 | tf_op jit(solution)/shard_map/reshape | solution.py:48
  572.1 18.5 %gather_fusion.1 = bf16[1152,2560]{1,0:T(8,128)(2,1)} fusion(bf16[2304,2560]{1,0:T(8,128)(2,1)} %reshape.111, s32[2048]{0:T(1024)S(1)} %pad_clamp_fusion.1), kind=kCustom, calls=%fused_computation.1 | custom fusion | bytes 11801088 | tf_op jit(solution)/shard_map/jit(_take)/gather | solution.py:49
  590.6 10.1 %gather.19 = bf16[192,6,2560]{2,1,0:T(8,128)(2,1)} reshape(bf16[1152,2560]{1,0:T(8,128)(2,1)} %gather_fusion.1) | data formatting | bytes 11796480 | tf_op jit(solution)/shard_map/jit(_take)/gather | solution.py:49
  600.7 10.6 %multiply_reduce_fusion = f32[192,2560]{1,0:T(8,128)S(1)} fusion(f32[192,6]{1,0:T(8,128)S(1)} %copy.57, bf16[192,6,2560]{2,1,0:T(8,128)(2,1)} %gather.19, pred[192,6]{1,0:T(8,128)(4,1)S(1)} %copy.47), kind=kLoop, calls=%fused_computation.4 | loop fusion | flops 11304960 | bytes 7870080 | tf_op jit(solution)/shard_map/reduce_sum | solution.py:50
  611.3 1.2 fusion.9
  (29 shorter events, 0.3 us)
Async XLA Ops:
  0.0 418.4 %copy-start = (bf16[2560,64]{0,1:T(8,128)(2,1)S(1)}, bf16[2560,64]{0,1:T(8,128)(2,1)}, u32[]{:S(2)}) copy-start(bf16[2560,64]{0,1:T(8,128)(2,1)} %param.9) | copy-start | bytes 983044
  21.3 0.6 copy-start.5
  21.9 8.7 %copy-start.7 = (s32[1152]{0:T(1024)}, s32[1152]{0:T(1024)S(1)}, u32[]{:S(2)}) copy-start(s32[1152]{0:T(1024)S(1)} %fusion.23) | copy-start | bytes 13828
  32.1 10.6 %copy-start.1 = (bf16[192,2560]{1,0:T(8,128)(2,1)}, bf16[192,2560]{1,0:T(8,128)(2,1)S(1)}, u32[]{:S(2)}) copy-start(bf16[192,2560]{1,0:T(8,128)(2,1)S(1)} %fusion.8) | copy-start | bytes 2949124
  411.4 6.6 %copy-start.6 = (s32[1152]{0:T(1024)S(1)}, s32[1152]{0:T(1024)}, u32[]{:S(2)}) copy-start(s32[1152]{0:T(1024)} %copy-done.5) | copy-start | bytes 13828
  411.4 6.7 %copy-start.4 = (s32[192,6]{0,1:T(8,128)S(1)}, s32[192,6]{0,1:T(8,128)}, u32[]{:S(2)}) copy-start(s32[192,6]{0,1:T(8,128)} %param.10) | copy-start | bytes 13828
  411.4 7.0 %copy-start.2 = (bf16[192,2560]{1,0:T(8,128)(2,1)S(1)}, bf16[192,2560]{1,0:T(8,128)(2,1)}, u32[]{:S(2)}) copy-start(bf16[192,2560]{1,0:T(8,128)(2,1)} %copy-done.1) | copy-start | bytes 2949124
  411.4 135.9 %all-to-all-start.1 = ((bf16[16,144,2560]{2,0,1:T(8,128)(2,1)}), bf16[16,144,2560]{2,0,1:T(8,128)(2,1)}, u32[]{:S(2)}, u32[]{:S(2)}) async-start(bf16[16,144,2560]{2,0,1:T(8,128)(2,1)} %copy.53), calls=%async_computation.1 | async-start | bytes 23592960 | tf_op jit(solution)/shard_map/all_to_all | solution.py:48
  419.0 10.0 %copy-start.8 = (s32[1152]{0:T(1024)S(1)}, s32[1152]{0:T(1024)}, u32[]{:S(2)}) copy-start(s32[1152]{0:T(1024)} %copy-done.7) | copy-start | bytes 13828
  590.6 20.7 %copy-start.3 = (bf16[192,2560]{1,0:T(8,128)(2,1)S(1)}, bf16[192,2560]{1,0:T(8,128)(2,1)}, u32[]{:S(2)}) copy-start(bf16[192,2560]{1,0:T(8,128)(2,1)} %param.7) | copy-start | bytes 2949124
where the time goes:
time: 614 us; the launch traced here: 613 us
  matrix products  172 us (28%)
  blocking collectives  148 us (24%)
  local copies, waits for them, and re-layouts  126 us (21%)
  waiting for transfers between devices  118 us (19%)
  other arithmetic  41.4 us (7%)
  starting transfers between devices  6.56 us (1%)
    all_to_all x1, blocking collectives, local_block(): received = lax.all_to_all(outgoing, 'ep', 0, 1, tiled=True)  148 us
    all_to_all x1, waiting for transfers between devices, local_block(): lax.all_to_all(outputs, 'ep', 1, 0, tiled=True)  118 us
    dot_general x1, matrix products, expert_mlp(): jnp.einsum('erd,edf->erf', rows, w_gate, preferred_element_type=jnp.float32)  62.8 us
    dot_general x1, matrix products, expert_mlp(): jnp.einsum('erd,edf->erf', rows, w_up, preferred_element_type=jnp.float32)  61.5 us
    dot_general x1, matrix products, expert_mlp(): jnp.einsum('erf,efd->erd', hidden_act, w_down, preferred_element_type=jnp...  47.1 us
    gather x2, local copies, waits for them, and re-layouts, local_block(): y_sel = jnp.take(returned, slots, axis=0).reshape(tokens, top_k, hidden)  28.6 us
    gather x2, local copies, waits for them, and re-layouts, local_block(): jnp.take(normed, slot_tok, axis=0, mode='fill', fill_value=0)  25.9 us
    another operation x3, other arithmetic  18.4 us
  transfers between devices with their start and end apart: 1, of which 1 were waited for; matrix products, arithmetic and copies ran while one was open for 2% of the time, Pallas kernels for 0%

commit v1 on v0

v1 whole, which is shorter than its diff:
```python
import functools

import jax
import jax.numpy as jnp
from jax import lax
from jax.experimental import pallas as pl
from jax.experimental.pallas import tpu as pltpu
from jax.sharding import PartitionSpec as P

EPS = 1e-6
TOK = 192
PAD = 256
CAP = 36
CROW = 2 * CAP
EROW = 4 * CAP
NE = 16
GE = 4
KC = 512
NK = 5
FF = 1536
NF = 3
NSLOT = 16
AHEAD = NSLOT // 2
P1 = NE * NK
P2 = NK * NE // 2
SLOTS = NE * CROW
f32, bf16, i32 = jnp.float32, jnp.bfloat16, jnp.int32


def kernel(x_hbm, gain_hbm, wr_hbm, ids_hbm, wg_hbm, wu_hbm, wd_hbm, out_ref,
           xv, gv, wrv, idv, h_all, info_own, info_all, gat, cmb, acc, act, ring, xg, yb, sib, rem,
           in_sem, ring_sem, h_send, h_recv, i_send, i_recv, s_send, s_recv, r_send, r_recv):
    me = lax.axis_index("ep")
    chip = me // 2
    core = me % 2
    sibling = chip * 2 + (1 - core)
    partner = (1 - chip) * 2 + core
    diag = (1 - chip) * 2 + (1 - core)

    ins = [pltpu.make_async_copy(s, d, in_sem.at[i]) for i, (s, d) in enumerate(
        ((x_hbm, xv), (gain_hbm, gv), (wr_hbm, wrv), (ids_hbm, idv)))]
    for c in ins:
        c.start()

    def start_p1(s):
        g = s // (NK * GE)
        k = (s % (NK * GE)) // GE
        e = g * GE + s % GE
        for m, w in enumerate((wg_hbm, wu_hbm)):
            slot = (2 * s + m) % NSLOT
            for n in range(NF):
                pltpu.make_async_copy(
                    w.at[e, pl.ds(k * KC, KC), pl.ds(n * KC, KC)],
                    ring.at[slot, pl.ds(n * KC, KC)], ring_sem.at[slot]).start()

    def start_p2(p):
        c = p // (NE // 2)
        j = p % (NE // 2)
        for m in range(2):
            slot = (2 * (P1 + p) + m) % NSLOT
            pltpu.make_async_copy(
                wd_hbm.at[2 * j + m, :, pl.ds(pl.multiple_of(c * KC, KC), KC)], ring.at[slot], ring_sem.at[slot]).start()

    def wait_slot(slot):
        pltpu.make_async_copy(wd_hbm.at[0, :, pl.ds(0, KC)], ring.at[slot], ring_sem.at[slot]).wait()

    for s in range(AHEAD):
        start_p1(s)

    barrier = pltpu.get_barrier_semaphore()
    for d in (sibling, partner, diag):
        pl.semaphore_signal(barrier, inc=1, device_id={"ep": d}, device_id_type=pl.DeviceIdType.MESH)

    for d in range(4):
        h_all[:, d * PAD + TOK:(d + 1) * PAD, :] = jnp.zeros((NK, PAD - TOK, KC), bf16)

    for c in ins:
        c.wait()
    my_rows = pl.ds(pl.multiple_of(me * PAD, PAD), TOK)
    ssq = jnp.zeros((TOK, 1), f32)
    for k in range(NK):
        xc = xv[:, k * KC:(k + 1) * KC].astype(f32)
        ssq = ssq + jnp.sum(xc * xc, axis=1, keepdims=True)
    inv = lax.rsqrt(ssq * (1.0 / (NK * KC)) + EPS)
    for k in range(NK):
        xc = xv[:, k * KC:(k + 1) * KC].astype(f32)
        h_all[k, my_rows, :] = (xc * inv * gv[:, k * KC:(k + 1) * KC].astype(f32)).astype(bf16)

    pl.semaphore_wait(barrier, 3)

    def h_copy(k, owner, target, ss, rs):
        rows = pl.ds(pl.multiple_of(owner * PAD, PAD), TOK)
        return pltpu.make_async_remote_copy(
            src_ref=h_all.at[k, rows], dst_ref=h_all.at[k, rows], send_sem=h_send.at[k, ss], recv_sem=h_recv.at[k, rs],
            device_id={"ep": target}, device_id_type=pl.DeviceIdType.MESH)

    for k in range(NK):
        h_copy(k, me, partner, 1, 1).start()
        h_copy(k, me, sibling, 0, 0).start()

    logits = jnp.zeros((64, TOK), f32)
    for k in range(NK):
        logits = logits + lax.dot_general(
            wrv[:, k * KC:(k + 1) * KC], h_all[k, my_rows, :], (((1,), (1,)), ((), ())), preferred_element_type=f32)
    e_iota = lax.broadcasted_iota(i32, (64, TOK), 0)
    hit = jnp.zeros((64, TOK), f32)
    for j in range(6):
        hit = hit + jnp.where(idv[j:j + 1, :] == e_iota, 1.0, 0.0)
    ex = jnp.exp(logits - jnp.max(logits, axis=0, keepdims=True))
    prob = ex / jnp.sum(ex, axis=0, keepdims=True)
    picked = prob * hit
    gates = picked / jnp.sum(picked, axis=0, keepdims=True)
    upper = (lax.broadcasted_iota(i32, (TOK, TOK), 0) < lax.broadcasted_iota(i32, (TOK, TOK), 1)).astype(f32).astype(bf16)
    before = jnp.dot(hit.astype(bf16), upper, preferred_element_type=f32)
    pos = jnp.where(hit > 0.5, before + (core * CAP).astype(f32), -1.0)
    for d in range(4):
        info_own[d, 0] = jnp.full((NE, PAD), -1.0, f32)
        info_own[d, 1] = jnp.zeros((NE, PAD), f32)
        info_own[d, 0, :, 0:TOK] = pos[d * NE:(d + 1) * NE]
        info_own[d, 1, :, 0:TOK] = gates[d * NE:(d + 1) * NE]

    def i_copy(idx, target):
        return pltpu.make_async_remote_copy(
            src_ref=info_own.at[target], dst_ref=info_all.at[me], send_sem=i_send.at[idx], recv_sem=i_recv.at[idx],
            device_id={"ep": target}, device_id_type=pl.DeviceIdType.MESH)

    peers = (sibling, partner, diag)
    for idx, d in enumerate(peers):
        i_copy(idx, d).start()
    info_all[me] = info_own[me]
    for idx, d in enumerate(peers):
        i_copy(idx, d).wait_recv()

    r_iota = lax.broadcasted_iota(i32, (CROW, 2 * PAD), 0).astype(f32)
    for ch in range(2):
        prow = jnp.concatenate([info_all[2 * ch, 0], info_all[2 * ch + 1, 0]], axis=1)
        for q in range(NE // 2):
            pair = [jnp.where(r_iota == prow[2 * q + i:2 * q + i + 1, :], 1.0, 0.0) for i in range(2)]
            gat[ch, q * EROW:(q + 1) * EROW, :] = jnp.concatenate(pair, axis=0).astype(bf16)

    acc[...] = jnp.zeros_like(acc)

    def build_combine():
        lane = lax.broadcasted_iota(i32, (NE, SLOTS), 1)
        expand = (lane // CROW == lax.broadcasted_iota(i32, (NE, SLOTS), 0)).astype(f32).astype(bf16)
        lane1 = lax.broadcasted_iota(i32, (TOK, SLOTS), 1)
        slot_r = (lane1 % CROW).astype(f32)
        for d in range(4):
            ptok = jnp.transpose(info_all[d, 0])[:TOK]
            wtok = jnp.transpose(info_all[d, 1])[:TOK]
            pexp = jnp.dot(ptok.astype(bf16), expand, preferred_element_type=f32)
            sel = pexp == slot_r
            rows = slice((d % 2) * TOK, (d % 2 + 1) * TOK)
            rest = wtok
            for i in range(3):
                part = rest.astype(bf16)
                rest = rest - part.astype(f32)
                wexp = jnp.dot(part, expand, preferred_element_type=f32)
                cmb[i, d // 2, rows, :] = jnp.where(sel, wexp, 0.0).astype(bf16)

    def k_body(gk, _):
        g = gk // NK
        k = gk % NK

        @pl.when(g == 0)
        def _():
            h_copy(k, partner, sibling, 1, 1).wait_recv()
            h_copy(k, partner, sibling, 2, 2).start()
            h_copy(k, sibling, sibling, 0, 0).wait_recv()
            h_copy(k, diag, sibling, 2, 2).wait_recv()

        outs = [jnp.dot(gat[ch, pl.ds(pl.multiple_of(g * (GE * CROW), GE * CROW), GE * CROW), :],
                        h_all[k, ch * 2 * PAD:(ch + 1) * 2 * PAD, :], preferred_element_type=f32) for ch in range(2)]
        for e in range(GE):
            xg[e] = jnp.concatenate([o[e * CROW:(e + 1) * CROW] for o in outs], axis=0).astype(bf16)

        def e_body(e, _):
            s = gk * GE + e
            xe = xg[e]
            for m in range(2):
                slot = (2 * s + m) % NSLOT
                wait_slot(slot)
                for n in range(NF):
                    rows = pl.ds(pl.multiple_of(((e * 2 + m) * NF + n) * EROW, EROW), EROW)
                    acc[rows, :] = acc[rows, :] + jnp.dot(
                        xe, ring[slot, n * KC:(n + 1) * KC, :], preferred_element_type=f32)

            @pl.when(s + AHEAD < P1)
            def _():
                start_p1(s + AHEAD)

            @pl.when(s + AHEAD >= P1)
            def _():
                start_p2(s + AHEAD - P1)
            return 0

        lax.fori_loop(0, GE, e_body, 0)

        @pl.when(k == NK - 1)
        def _():
            def s_body(e, _):
                for n in range(NF):
                    rg = pl.ds(pl.multiple_of(((e * 2) * NF + n) * EROW, EROW), EROW)
                    ru = pl.ds(pl.multiple_of(((e * 2 + 1) * NF + n) * EROW, EROW), EROW)
                    a = jax.nn.silu(acc[rg, :]) * acc[ru, :]
                    act[g * GE + e, :, n * KC:(n + 1) * KC] = a.astype(bf16)
                    acc[rg, :] = jnp.zeros((EROW, KC), f32)
                    acc[ru, :] = jnp.zeros((EROW, KC), f32)
                return 0
            lax.fori_loop(0, GE, s_body, 0)

        @pl.when(gk == 2 * NK)
        def _():
            build_combine()
        return 0

    lax.fori_loop(0, (NE // GE) * NK, k_body, 0)

    def part_rows(slot, mine_chip, which):
        return pl.ds(pl.multiple_of(((slot * 2 + mine_chip) * 2 + which) * TOK, TOK), TOK)

    def s_copy(c, i):
        return pltpu.make_async_remote_copy(
            src_ref=acc.at[part_rows(c % 2, i, 1 - core)], dst_ref=sib.at[c, i],
            send_sem=s_send.at[c, i], recv_sem=s_recv.at[c, i],
            device_id={"ep": sibling}, device_id_type=pl.DeviceIdType.MESH)

    def r_copy(c):
        return pltpu.make_async_remote_copy(
            src_ref=sib.at[c, 0], dst_ref=rem.at[c], send_sem=r_send.at[c], recv_sem=r_recv.at[c],
            device_id={"ep": partner}, device_id_type=pl.DeviceIdType.MESH)

    def relay(c):
        s_copy(c, 0).wait_recv()
        sib[c, 0] = sib[c, 0] + acc[part_rows(c % 2, 0, core), :]
        r_copy(c).start()
        s_copy(c, 1).wait_recv()
        sib[c, 1] = sib[c, 1] + acc[part_rows(c % 2, 1, core), :]

    def combine(c):
        @pl.when(c >= 2)
        def _():
            s_copy(c - 2, 0).wait_send()
            s_copy(c - 2, 1).wait_send()
        for i in range(2):
            ch = (1 - chip) if i == 0 else chip
            tot = jnp.zeros((2 * TOK, KC), f32)
            for q in range(3):
                tot = tot + jnp.dot(cmb[q, ch], yb[ch], preferred_element_type=f32)
            acc[pl.ds(pl.multiple_of(((c % 2) * 2 + i) * 2 * TOK, 2 * TOK), 2 * TOK), :] = tot
            s_copy(c, i).start()

    def d_body(p, _):
        c = p // (NE // 2)
        j = p % (NE // 2)
        ys = []
        for m in range(2):
            slot = (2 * (P1 + p) + m) % NSLOT
            wait_slot(slot)
            ys.append(jnp.dot(act[2 * j + m], ring[slot], preferred_element_type=f32))
        for ch in range(2):
            yb[ch, pl.ds(pl.multiple_of(j * EROW, EROW), EROW), :] = jnp.concatenate(
                [y[ch * CROW:(ch + 1) * CROW] for y in ys], axis=0).astype(bf16)

        @pl.when(p + AHEAD < P2)
        def _():
            start_p2(p + AHEAD)

        @pl.when((j == 1) & (c > 0))
        def _():
            relay(c - 1)

        @pl.when(j == NE // 2 - 1)
        def _():
            combine(c)
        return 0

    lax.fori_loop(0, P2, d_body, 0)
    relay(NK - 1)

    for c in range(NK):
        r_copy(c).wait_recv()
        cols = slice(c * KC, (c + 1) * KC)
        out_ref[:, cols] = (xv[:, cols].astype(f32) + (sib[c, 1] + rem[c])).astype(bf16)

    for k in range(NK):
        h_copy(k, me, sibling, 0, 0).wait_send()
        h_copy(k, me, partner, 1, 1).wait_send()
        h_copy(k, partner, sibling, 2, 2).wait_send()
    for idx, d in enumerate(peers):
        i_copy(idx, d).wait_send()
    for c in range(NK):
        r_copy(c).wait_send()
    for c in range(NK - 2, NK):
        for i in range(2):
            s_copy(c, i).wait_send()


def solution(mesh):
    def local_block(x_in, norm_gain, w_router, expert_ids, w_gate, w_up, w_down):
        tokens, hidden = x_in.shape
        dma = pltpu.SemaphoreType.DMA
        return pl.pallas_call(
            kernel,
            out_shape=jax.ShapeDtypeStruct((tokens, hidden), bf16),
            in_specs=[pl.BlockSpec(memory_space=pl.ANY)] * 7,
            out_specs=pl.BlockSpec(memory_space=pltpu.VMEM),
            scratch_shapes=[
                pltpu.VMEM((TOK, NK * KC), bf16),
                pltpu.VMEM((1, NK * KC), bf16),
                pltpu.VMEM((64, NK * KC), bf16),
                pltpu.VMEM((6, TOK), i32),
                pltpu.VMEM((NK, 4 * PAD, KC), bf16),
                pltpu.VMEM((4, 2, NE, PAD), f32),
                pltpu.VMEM((4, 2, NE, PAD), f32),
                pltpu.VMEM((2, SLOTS, 2 * PAD), bf16),
                pltpu.VMEM((3, 2, 2 * TOK, SLOTS), bf16),
                pltpu.VMEM((GE * 2 * NF * EROW, KC), f32),
                pltpu.VMEM((NE, EROW, FF), bf16),
                pltpu.VMEM((NSLOT, FF, KC), bf16),
                pltpu.VMEM((GE, EROW, KC), bf16),
                pltpu.VMEM((2, SLOTS, KC), bf16),
                pltpu.VMEM((NK, 2, TOK, KC), f32),
                pltpu.VMEM((NK, TOK, KC), f32),
                dma((4,)), dma((NSLOT,)),
                dma((NK, 3)), dma((NK, 3)),
                dma((3,)), dma((3,)),
                dma((NK, 2)), dma((NK, 2)),
                dma((NK,)), dma((NK,)),
            ],
            compiler_params=pltpu.CompilerParams(
                collective_id=0, has_side_effects=True, vmem_limit_bytes=67_043_328),
            name="moe_step",
        )(x_in, norm_gain.reshape(1, hidden), w_router.T, expert_ids.T, w_gate, w_up, w_down)

    tok_spec = P(("dp", "ep"), None)
    expert_spec = P("ep", None, None)
    return jax.shard_map(local_block, mesh=mesh, in_specs=(tok_spec, P(None), P(None, None), tok_spec, expert_spec, expert_spec, expert_spec), out_specs=tok_spec, check_vma=False)
```

time: 614 us -> 189 us (0.31)
  Pallas kernels: 0 us -> 186 us
  matrix products: 172 us -> 0 us
  blocking collectives: 148 us -> 0 us
  local copies, waits for them, and re-layouts: 126 us -> 3.51 us
  waiting for transfers between devices: 118 us -> 0 us
  other arithmetic: 41.4 us -> 0 us
  starting transfers between devices: 6.56 us -> 0 us
    pallas_call x0 -> x1, Pallas kernels: none -> 186 us  [local_block(): pl.pallas_call(kernel, out_shape=jax.ShapeDtypeStruct((tokens, hidden), b...]
    dot_general x4 -> x0, matrix products: 172 us -> none  [the longest x1 62.8 us: expert_mlp(): jnp.einsum('erd,edf->erf', rows, w_gate, preferred_element_type=jnp.float32)]
    all_to_all x1 -> x0, blocking collectives: 148 us -> none  [local_block(): received = lax.all_to_all(outgoing, 'ep', 0, 1, tiled=True)]
    all_to_all x1 -> x0, waiting for transfers between devices: 118 us -> none  [local_block(): lax.all_to_all(outputs, 'ep', 1, 0, tiled=True)]
    gather x9 -> x0, local copies, waits for them, and re-layouts: 64.3 us -> none  [the longest x2 28.6 us: local_block(): y_sel = jnp.take(returned, slots, axis=0).reshape(tokens, top_k, hidden)]
    all_to_all x2 -> x0, local copies, waits for them, and re-layouts: 19.2 us -> none  [the longest x1 10 us: local_block(): lax.all_to_all(outputs, 'ep', 1, 0, tiled=True)]
    another operation x3 -> x0, other arithmetic: 18.4 us -> none
    convert_element_type x1 -> x0, local copies, waits for them, and re-layouts: 18.1 us -> none  [expert_mlp(): jnp.einsum('erf,efd->erd', hidden_act, w_down, preferred_element_type=jnp...]
  transfers between devices with their start and end apart: 1 -> 0, of which waited for: 1 -> 0; matrix products, arithmetic and copies ran while one was open for 2% -> 0% of each run, Pallas kernels for 0% -> 0%
where the time goes in v1:
time: 189 us
  Pallas kernels  186 us (98%)
  local copies, waits for them, and re-layouts  3.51 us (2%)
    pallas_call x1, Pallas kernels, local_block(): pl.pallas_call(kernel, out_shape=jax.ShapeDtypeStruct((tokens, hidden), b...  186 us

profile of v1, /device:TPU:0, one launch (start us, length us, event | category | flops | bytes accessed | tf_op | source)
XLA Modules:
  0.0 189.2 jit_solution(6532791568616793041)
XLA Ops:
  0.0 1.3 reshape.3.gain_hbm
  1.3 185.7 %moe_step.1 = bf16[192,2560]{1,0:T(8,128)(2,1)} custom-call(bf16[192,2560]{1,0:T(8,128)(2,1)} %x_hbm.1, bf16[1,2560]{1,0:T(2,128)(2,1)} %reshape.3.gain_hbm, bf16[64,2560]{1,0:T(8,128)(2,1)} %bitcast.2, s32[6,192]{1,0:T(8,128)} %bitcast.3, bf16[16,2560,1536]{2,1,0:T(8,128)(2,1)} %wg_hbm.1, bf16[16,2560,1536]{2,1,0:T(8,128)(2,1)} %wu_hbm.1, ...), custom_call_target="tpu_custom_call" | custom-call | tf_op jit(solution)/shard_map/moe_step/pallas_call | solution.py:303
  187.0 2.2 %copy.9 = bf16[192,2560]{1,0:T(8,128)(2,1)} copy(bf16[192,2560]{1,0:T(8,128)(2,1)} %moe_step.1) | data formatting | bytes 1966080

commit v2 on v1

v2 whole, which is shorter than its diff:
```python
import functools

import jax
import jax.numpy as jnp
from jax import lax
from jax.experimental import pallas as pl
from jax.experimental.pallas import tpu as pltpu
from jax.sharding import PartitionSpec as P

EPS = 1e-6
TOK = 192
PAD = 256
CAP = 36
EROW = 4 * CAP
NE = 16
GE = 4
KC = 512
NK = 5
FF = 1536
NF = 3
NSLOT = 16
AHEAD = NSLOT // 2
P1 = NE * NK
P2 = NK * NE // 2
PROW = 2 * CAP
DSLOT = NE // 2 * PROW
MISS = -100.0
f32, bf16, i32 = jnp.float32, jnp.bfloat16, jnp.int32


def kernel(x_hbm, gain_hbm, wr_hbm, ids_hbm, wg_hbm, wu_hbm, wd_hbm, out_ref,
           xv, gv, wrv, idv, h_all, pos_own, gate_own, pos_all, gate_all, gat, cmb, acc, act, ring, xg, yb, sib, rem,
           in_sem, ring_sem, h_send, h_recv, p_send, p_recv, g_send, g_recv, s_send, s_recv, r_send, r_recv):
    me = lax.axis_index("ep")
    chip = me // 2
    core = me % 2
    sibling = chip * 2 + (1 - core)
    partner = (1 - chip) * 2 + core
    diag = (1 - chip) * 2 + (1 - core)
    peers = (partner, diag, sibling)

    ins = [pltpu.make_async_copy(s, d, in_sem.at[i]) for i, (s, d) in enumerate(
        ((ids_hbm, idv), (x_hbm, xv), (gain_hbm, gv), (wr_hbm, wrv)))]
    for c in ins:
        c.start()

    def start_p1(s):
        g = s // (NK * GE)
        k = (s % (NK * GE)) // GE
        e = g * GE + s % GE
        for m, w in enumerate((wg_hbm, wu_hbm)):
            slot = (2 * s + m) % NSLOT
            for n in range(NF):
                pltpu.make_async_copy(
                    w.at[e, pl.ds(k * KC, KC), pl.ds(n * KC, KC)],
                    ring.at[slot, pl.ds(n * KC, KC)], ring_sem.at[slot]).start()

    def start_p2(p):
        c = p // (NE // 2)
        j = p % (NE // 2)
        for m in range(2):
            slot = (2 * (P1 + p) + m) % NSLOT
            pltpu.make_async_copy(
                wd_hbm.at[2 * j + m, :, pl.ds(pl.multiple_of(c * KC, KC), KC)], ring.at[slot], ring_sem.at[slot]).start()

    def wait_slot(slot):
        pltpu.make_async_copy(wd_hbm.at[0, :, pl.ds(0, KC)], ring.at[slot], ring_sem.at[slot]).wait()

    barrier = pltpu.get_barrier_semaphore()
    for d in peers:
        pl.semaphore_signal(barrier, inc=1, device_id={"ep": d}, device_id_type=pl.DeviceIdType.MESH)

    for d in range(4):
        h_all[:, d * PAD + TOK:(d + 1) * PAD, :] = jnp.zeros((NK, PAD - TOK, KC), bf16)
    for d in range(4):
        pos_own[d] = jnp.full((NE, PAD), MISS, f32)
        gate_own[d] = jnp.zeros((NE, PAD), f32)

    ins[0].wait()
    e_iota = lax.broadcasted_iota(i32, (64, TOK), 0)
    hit = jnp.zeros((64, TOK), f32)
    for j in range(6):
        hit = hit + jnp.where(idv[j:j + 1, :] == e_iota, 1.0, 0.0)
    upper = (lax.broadcasted_iota(i32, (TOK, TOK), 0) < lax.broadcasted_iota(i32, (TOK, TOK), 1)).astype(f32).astype(bf16)
    before = jnp.dot(hit.astype(bf16), upper, preferred_element_type=f32)
    pos = jnp.where(hit > 0.5, before, MISS)
    for d in range(4):
        pos_own[d, :, 0:TOK] = pos[d * NE:(d + 1) * NE]

    for c in ins[1:]:
        c.wait()
    for s in range(AHEAD):
        start_p1(s)
    my_rows = pl.ds(pl.multiple_of(me * PAD, PAD), TOK)
    ssq = jnp.zeros((TOK, 1), f32)
    for k in range(NK):
        xc = xv[:, k * KC:(k + 1) * KC].astype(f32)
        ssq = ssq + jnp.sum(xc * xc, axis=1, keepdims=True)
    inv = lax.rsqrt(ssq * (1.0 / (NK * KC)) + EPS)
    for k in range(NK):
        xc = xv[:, k * KC:(k + 1) * KC].astype(f32)
        h_all[k, my_rows, :] = (xc * inv * gv[:, k * KC:(k + 1) * KC].astype(f32)).astype(bf16)

    pl.semaphore_wait(barrier, 3)

    def small_copy(own, everyone, ss, rs, idx, target):
        return pltpu.make_async_remote_copy(
            src_ref=own.at[target], dst_ref=everyone.at[me], send_sem=ss.at[idx], recv_sem=rs.at[idx],
            device_id={"ep": target}, device_id_type=pl.DeviceIdType.MESH)

    def pos_copy(idx):
        return small_copy(pos_own, pos_all, p_send, p_recv, idx, peers[idx])

    def gate_copy(idx):
        return small_copy(gate_own, gate_all, g_send, g_recv, idx, peers[idx])

    def h_copy(k, owner, target, ss):
        rows = pl.ds(pl.multiple_of(owner * PAD, PAD), TOK)
        return pltpu.make_async_remote_copy(
            src_ref=h_all.at[k, rows], dst_ref=h_all.at[k, rows], send_sem=h_send.at[k, ss], recv_sem=h_recv.at[k, ss],
            device_id={"ep": target}, device_id_type=pl.DeviceIdType.MESH)

    def own_to_sibling(k):
        return h_copy(k, me, sibling, 0)

    def own_to_partner(k):
        return h_copy(k, me, partner, 1)

    def hand_on(k):
        return h_copy(k, partner, sibling, 2)

    for idx in range(3):
        pos_copy(idx).start()
    for k in range(NK):
        own_to_partner(k).start()
        own_to_sibling(k).start()

    logits = jnp.zeros((64, TOK), f32)
    for k in range(NK):
        logits = logits + lax.dot_general(
            wrv[:, k * KC:(k + 1) * KC], h_all[k, my_rows, :], (((1,), (1,)), ((), ())), preferred_element_type=f32)
    ex = jnp.exp(logits - jnp.max(logits, axis=0, keepdims=True))
    prob = ex / jnp.sum(ex, axis=0, keepdims=True)
    picked = prob * hit
    gates = picked / jnp.sum(picked, axis=0, keepdims=True)
    for d in range(4):
        gate_own[d, :, 0:TOK] = gates[d * NE:(d + 1) * NE]
    for idx in range(3):
        gate_copy(idx).start()
    pos_all[me] = pos_own[me]
    gate_all[me] = gate_own[me]
    acc[...] = jnp.zeros_like(acc)

    for idx in range(3):
        pos_copy(idx).wait_recv()

    ri = lax.broadcasted_iota(i32, (PROW, PAD), 0)
    r_iota = ri.astype(f32)
    low = ri < CAP
    for d in range(4):
        for q in range(NE // 4):
            two = []
            for jj in range(2):
                e0 = 4 * q + 2 * jj
                ea, eb = e0 + d % 2, e0 + 1 - d % 2
                want = jnp.where(low, pos_all[d, ea:ea + 1, :], pos_all[d, eb:eb + 1, :] + CAP)
                two.append(jnp.where(r_iota == want, 1.0, 0.0))
            gat[d, q * EROW:(q + 1) * EROW, :] = jnp.concatenate(two, axis=0).astype(bf16)

    own_to_partner(0).wait_recv()
    hand_on(0).start()

    def build_combine():
        for idx in range(3):
            gate_copy(idx).wait_recv()
        le = lax.broadcasted_iota(i32, (NE, DSLOT), 1)
        ee = lax.broadcasted_iota(i32, (NE, DSLOT), 0)
        lane = lax.broadcasted_iota(i32, (TOK, DSLOT), 1) % PROW
        slot_r = jnp.where(lane < CAP, lane, lane - CAP).astype(f32)
        for d in range(4):
            swap = jnp.where(le % PROW < CAP, d % 2, 1 - d % 2)
            expand = (le // PROW * 2 + swap == ee).astype(f32).astype(bf16)
            ptok = jnp.transpose(pos_all[d])[:TOK]
            wtok = jnp.transpose(gate_all[d])[:TOK]
            pexp = jnp.dot(ptok.astype(bf16), expand, preferred_element_type=f32)
            sel = pexp == slot_r
            rest = wtok
            for i in range(3):
                part = rest.astype(bf16)
                rest = rest - part.astype(f32)
                wexp = jnp.dot(part, expand, preferred_element_type=f32)
                cmb[d, i] = jnp.where(sel, wexp, 0.0).astype(bf16)

    half = lax.broadcasted_iota(i32, (PROW, KC), 0) < CAP

    def k_body(gk, _):
        g = gk // NK
        k = gk % NK

        @pl.when(g == 0)
        def _():
            own_to_sibling(k).wait_recv()
            hand_on(k).wait_recv()

        outs = [jnp.dot(gat[d, pl.ds(pl.multiple_of(g * EROW, EROW), EROW), :],
                        h_all[k, d * PAD:(d + 1) * PAD, :], preferred_element_type=f32) for d in range(4)]
        for jj in range(2):
            o = [v[jj * PROW:(jj + 1) * PROW] for v in outs]
            xg[2 * jj] = jnp.concatenate(
                [jnp.where(half, o[0], o[1]), jnp.where(half, o[2], o[3])], axis=0).astype(bf16)
            xg[2 * jj + 1] = jnp.concatenate(
                [jnp.where(half, o[1], o[0]), jnp.where(half, o[3], o[2])], axis=0).astype(bf16)

        for jj in range(GE // 2):
            s0 = gk * GE + 2 * jj
            for i in range(4):
                wait_slot((2 * s0 + i) % NSLOT)
            for i in range(2):
                e = 2 * jj + i
                for m in range(2):
                    slot = (2 * s0 + 2 * i + m) % NSLOT
                    for n in range(NF):
                        r = ((e * 2 + m) * NF + n) * EROW
                        acc[r:r + EROW, :] = acc[r:r + EROW, :] + jnp.dot(
                            xg[e], ring[slot, n * KC:(n + 1) * KC, :], preferred_element_type=f32)

            for i in range(2):
                s = s0 + i

                @pl.when(s + AHEAD < P1)
                def _():
                    start_p1(s + AHEAD)

                @pl.when(s + AHEAD >= P1)
                def _():
                    start_p2(s + AHEAD - P1)

            if jj == 0:
                @pl.when(gk < NK - 1)
                def _():
                    own_to_partner(k + 1).wait_recv()
                    hand_on(k + 1).start()

        @pl.when(k == NK - 1)
        def _():
            def s_body(e, _):
                for n in range(NF):
                    rg = pl.ds(pl.multiple_of(((e * 2) * NF + n) * EROW, EROW), EROW)
                    ru = pl.ds(pl.multiple_of(((e * 2 + 1) * NF + n) * EROW, EROW), EROW)
                    a = jax.nn.silu(acc[rg, :]) * acc[ru, :]
                    act[g * GE + e, :, n * KC:(n + 1) * KC] = a.astype(bf16)
                    acc[rg, :] = jnp.zeros((EROW, KC), f32)
                    acc[ru, :] = jnp.zeros((EROW, KC), f32)
                return 0
            lax.fori_loop(0, GE, s_body, 0)

        @pl.when(gk == 2 * NK)
        def _():
            build_combine()
        return 0

    lax.fori_loop(0, (NE // GE) * NK, k_body, 0)

    def part_rows(slot, where, which):
        return pl.ds(pl.multiple_of(((slot * 2 + where) * 2 + which) * TOK, TOK), TOK)

    def s_copy(c, i):
        return pltpu.make_async_remote_copy(
            src_ref=acc.at[part_rows(c % 2, i, 1 - core)], dst_ref=sib.at[c, i],
            send_sem=s_send.at[c, i], recv_sem=s_recv.at[c, i],
            device_id={"ep": sibling}, device_id_type=pl.DeviceIdType.MESH)

    def r_copy(c):
        return pltpu.make_async_remote_copy(
            src_ref=sib.at[c, 0], dst_ref=rem.at[c], send_sem=r_send.at[c], recv_sem=r_recv.at[c],
            device_id={"ep": partner}, device_id_type=pl.DeviceIdType.MESH)

    def relay(c):
        s_copy(c, 0).wait_recv()
        sib[c, 0] = sib[c, 0] + acc[part_rows(c % 2, 0, core), :]
        r_copy(c).start()
        s_copy(c, 1).wait_recv()
        sib[c, 1] = sib[c, 1] + acc[part_rows(c % 2, 1, core), :]

    def combine(c):
        @pl.when(c >= 2)
        def _():
            s_copy(c - 2, 0).wait_send()
            s_copy(c - 2, 1).wait_send()
        for i in range(2):
            ch = (1 - chip) if i == 0 else chip
            for w in range(2):
                d = ch * 2 + w
                tot = jnp.dot(cmb[d, 0], yb[d], preferred_element_type=f32)
                for q in range(1, 3):
                    tot = tot + jnp.dot(cmb[d, q], yb[d], preferred_element_type=f32)
                acc[part_rows(c % 2, i, w), :] = tot
            s_copy(c, i).start()

    def d_body(t, _):
        c = t // (NE // 4)
        q = t % (NE // 4)
        ys = []
        for i in range(4):
            wait_slot((2 * P1 + 4 * t + i) % NSLOT)
        for i in range(4):
            ys.append(jnp.dot(act[4 * q + i], ring[(2 * P1 + 4 * t + i) % NSLOT], preferred_element_type=f32))
        for ch in range(2):
            r0, r1 = ch * PROW, (ch + 1) * PROW
            for w in range(2):
                rows = [jnp.where(half, ys[2 * jj + w][r0:r1], ys[2 * jj + 1 - w][r0:r1]) for jj in range(2)]
                yb[2 * ch + w, pl.ds(pl.multiple_of(q * EROW, EROW), EROW), :] = jnp.concatenate(
                    rows, axis=0).astype(bf16)

        for i in range(2):
            p = 2 * t + i

            @pl.when(p + AHEAD < P2)
            def _():
                start_p2(p + AHEAD)

        @pl.when((q == 0) & (c > 0))
        def _():
            relay(c - 1)

        @pl.when(q == NE // 4 - 1)
        def _():
            combine(c)
        return 0

    lax.fori_loop(0, P2 // 2, d_body, 0)
    relay(NK - 1)

    for c in range(NK):
        r_copy(c).wait_recv()
        cols = slice(c * KC, (c + 1) * KC)
        out_ref[:, cols] = (xv[:, cols].astype(f32) + (sib[c, 1] + rem[c])).astype(bf16)

    for k in range(NK):
        own_to_sibling(k).wait_send()
        own_to_partner(k).wait_send()
        hand_on(k).wait_send()
    for idx in range(3):
        pos_copy(idx).wait_send()
        gate_copy(idx).wait_send()
    for c in range(NK):
        r_copy(c).wait_send()
    for c in range(NK - 2, NK):
        for i in range(2):
            s_copy(c, i).wait_send()


def solution(mesh):
    def local_block(x_in, norm_gain, w_router, expert_ids, w_gate, w_up, w_down):
        tokens, hidden = x_in.shape
        dma = pltpu.SemaphoreType.DMA
        return pl.pallas_call(
            kernel,
            out_shape=jax.ShapeDtypeStruct((tokens, hidden), bf16),
            in_specs=[pl.BlockSpec(memory_space=pl.ANY)] * 7,
            out_specs=pl.BlockSpec(memory_space=pltpu.VMEM),
            scratch_shapes=[
                pltpu.VMEM((TOK, NK * KC), bf16),
                pltpu.VMEM((1, NK * KC), bf16),
                pltpu.VMEM((64, NK * KC), bf16),
                pltpu.VMEM((6, TOK), i32),
                pltpu.VMEM((NK, 4 * PAD, KC), bf16),
                pltpu.VMEM((4, NE, PAD), f32),
                pltpu.VMEM((4, NE, PAD), f32),
                pltpu.VMEM((4, NE, PAD), f32),
                pltpu.VMEM((4, NE, PAD), f32),
                pltpu.VMEM((4, DSLOT, PAD), bf16),
                pltpu.VMEM((4, 3, TOK, DSLOT), bf16),
                pltpu.VMEM((GE * 2 * NF * EROW, KC), f32),
                pltpu.VMEM((NE, EROW, FF), bf16),
                pltpu.VMEM((NSLOT, FF, KC), bf16),
                pltpu.VMEM((GE, EROW, KC), bf16),
                pltpu.VMEM((4, DSLOT, KC), bf16),
                pltpu.VMEM((NK, 2, TOK, KC), f32),
                pltpu.VMEM((NK, TOK, KC), f32),
                dma((4,)), dma((NSLOT,)),
                dma((NK, 3)), dma((NK, 3)),
                dma((3,)), dma((3,)),
                dma((3,)), dma((3,)),
                dma((NK, 2)), dma((NK, 2)),
                dma((NK,)), dma((NK,)),
            ],
            compiler_params=pltpu.CompilerParams(
                collective_id=0, has_side_effects=True, vmem_limit_bytes=67_043_328),
            name="moe_step",
        )(x_in, norm_gain.reshape(1, hidden), w_router.T, expert_ids.T, w_gate, w_up, w_down)

    tok_spec = P(("dp", "ep"), None)
    expert_spec = P("ep", None, None)
    return jax.shard_map(local_block, mesh=mesh, in_specs=(tok_spec, P(None), P(None, None), tok_spec, expert_spec, expert_spec, expert_spec), out_specs=tok_spec, check_vma=False)
```

time: 189 us -> 145 us (0.77)
  Pallas kernels: 186 us -> 141 us
    pallas_call x1, Pallas kernels: 186 us -> 141 us  [local_block(): pl.pallas_call(kernel, out_shape=jax.ShapeDtypeStruct((tokens, hidden), b...]
where the time goes in v2:
time: 145 us
  Pallas kernels  141 us (97%)
  local copies, waits for them, and re-layouts  3.51 us (2%)
    pallas_call x1, Pallas kernels, local_block(): pl.pallas_call(kernel, out_shape=jax.ShapeDtypeStruct((tokens, hidden), b...  141 us

profile of v2, /device:TPU:0, one launch (start us, length us, event | category | flops | bytes accessed | tf_op | source)
XLA Modules:
  0.0 144.5 jit_solution(13062609635317229198)
XLA Ops:
  0.0 1.3 reshape.3.gain_hbm
  1.3 141.0 %moe_step.1 = bf16[192,2560]{1,0:T(8,128)(2,1)} custom-call(bf16[192,2560]{1,0:T(8,128)(2,1)} %x_hbm.1, bf16[1,2560]{1,0:T(2,128)(2,1)} %reshape.3.gain_hbm, bf16[64,2560]{1,0:T(8,128)(2,1)} %bitcast.2, s32[6,192]{1,0:T(8,128)} %bitcast.3, bf16[16,2560,1536]{2,1,0:T(8,128)(2,1)} %wg_hbm.1, bf16[16,2560,1536]{2,1,0:T(8,128)(2,1)} %wu_hbm.1, ...), custom_call_target="tpu_custom_call" | custom-call | tf_op jit(solution)/shard_map/moe_step/pallas_call | solution.py:357
  142.3 2.2 %copy.9 = bf16[192,2560]{1,0:T(8,128)(2,1)} copy(bf16[192,2560]{1,0:T(8,128)(2,1)} %moe_step.1) | data formatting | bytes 1966080
